TPU v7x, 32 devices: a whole 2x2x4 slice. The times are simulated.
32 devices in a mesh: rep: 4 (over y, x), dom: 8 (over z, core).
Axes of the slice: x: 2, y: 2, z: 4, core: 2. Of those that a mesh axis runs over, the one named last changes fastest.
Arguments:
- node_pos: float32 [3, 16384], P(None, 'dom'), may hold values from -6 to 6
- node_order: int32 [8, 2048], P('dom'), may hold values from 0 to 2047, each once within a row
- facet_centroid: float32 [3, 16384], P(None, 'dom'), may hold values from -6 to 6
- facet_normal: float32 [3, 16384], P(None, 'dom'), may hold values from -6 to 6
- facet_nodes: int32 [3, 16384], P(None, 'dom'), may hold values from 0 to 2047
- pair_bucket: int32 [4, 8, 128], P('rep', 'dom'), may hold values from 0 to 15
- pair_owner: int32 [4, 8, 128, 1], P('rep', 'dom'), may hold values from 0 to 7; in each aligned block of 128 rows (0 to 127, 128 to 255, ..., all dimensions but the last counted through in order) at most 32 rows name the same one
- pair_slot: int32 [4, 8, 128], P('rep', 'dom'), may hold values from 0 to 15
- pair_count: int32 [4, 8], P('rep', 'dom'), may hold values from 64 to 128, as said below
Outputs:
- node_force: float32 [3, 16384], P(None, 'dom')
Inputs may be any that keep to these rules, and one draw needn't show every extreme that they name: `pair_owner`: among the 128 pairs of one device, each domain is named at most 32 times, and exactly 32 times in some device's pairs. `pair_count`: some device uses all 128 pairs. `node_order`: each row is a permutation.
All inputs are finite; a program needn't handle non-finite values.
Results may differ from a plain program's by a relative error of at most 0.00013.
Values sent between devices are 32-bit elements; how exact they have to be, the bound alone decides.
A program may use at most 64 MiB of HBM per device.

v0:
```python
import jax
import jax.numpy as jnp
from jax import lax
from jax.sharding import PartitionSpec as P

BUCKET = 128
PAIRS_DEV = 128
STIFFNESS = 0.125
RADIUS_SQ = 4.0
pair_block = 8


def tile_terms(facet_geom, node_points):
    centre = facet_geom[:, 0:3]
    normal = facet_geom[:, 3:6]
    delta = node_points[:, :, None, :] - centre[:, :, :, None]
    gap = jnp.sum(normal[:, :, :, None] * delta, axis=1)
    dist = jnp.sum(delta * delta, axis=1)
    strength = STIFFNESS * jax.nn.softplus(-gap) * jnp.exp(-dist / RADIUS_SQ)
    node_term = jnp.einsum("bkf,bfp->bkp", normal, strength, precision=lax.Precision.HIGHEST)
    reaction = -normal * jnp.sum(strength, axis=2)[:, None, :]
    return (node_term, reaction)


def slot_numbers(owners, is_live, per_owner, dummy_slot):
    rows = owners.shape[0]
    positions = jnp.arange(rows, dtype=jnp.int32)
    earlier = (
        (positions[None, :] < positions[:, None])
        & (owners[None, :] == owners[:, None])
        & is_live[None, :]
    )
    ranking = jnp.sum(earlier.astype(jnp.int32), axis=1)
    return jnp.where(is_live, owners * per_owner + ranking, dummy_slot)


def pair_loop(
    live_count, geom_rows, point_rows, slot_index, bucket_index, is_live, slot_total, bucket_total
):
    width = geom_rows.shape[2]
    geom_pad = jnp.concatenate([geom_rows, jnp.zeros((pair_block, 6, width), jnp.float32)], 0)
    point_pad = jnp.concatenate([point_rows, jnp.zeros((pair_block, 3, width), jnp.float32)], 0)
    slot_pad = jnp.concatenate([slot_index, jnp.full((pair_block,), slot_total, jnp.int32)])
    bucket_pad = jnp.concatenate([bucket_index, jnp.zeros((pair_block,), jnp.int32)])
    live_pad = jnp.concatenate([is_live, jnp.zeros((pair_block,), jnp.bool_)])

    def step(block_index, carry):
        slot_acc, bucket_acc = carry
        start = block_index * pair_block
        facet_geom = lax.dynamic_slice_in_dim(geom_pad, start, pair_block)
        node_points = lax.dynamic_slice_in_dim(point_pad, start, pair_block)
        slot_take = lax.dynamic_slice_in_dim(slot_pad, start, pair_block)
        bucket_take = lax.dynamic_slice_in_dim(bucket_pad, start, pair_block)
        weight = lax.dynamic_slice_in_dim(live_pad, start, pair_block).astype(jnp.float32)
        node_term, reaction = tile_terms(facet_geom, node_points)
        slot_acc = slot_acc.at[slot_take].add(node_term * weight[:, None, None])
        bucket_acc = bucket_acc.at[bucket_take].add(reaction * weight[:, None, None])
        return (slot_acc, bucket_acc)

    blocks = (live_count + pair_block - 1) // pair_block
    start_acc = (
        jnp.zeros((slot_total + 1, 3, width), jnp.float32),
        jnp.zeros((bucket_total, 3, width), jnp.float32),
    )
    return lax.fori_loop(jnp.int32(0), blocks, step, start_acc)


def per_device(
    node_pos,
    node_order,
    facet_centroid,
    facet_normal,
    facet_nodes,
    pair_bucket,
    pair_owner,
    pair_slot,
    pair_count,
):
    domains = lax.axis_size("dom")
    per_owner = max(2, 2 * PAIRS_DEV // domains)
    slot_total = domains * per_owner
    width = BUCKET
    node_buckets = node_pos.shape[1] // width
    facet_buckets = facet_centroid.shape[1] // width
    bucket_points = node_pos[:, node_order[0]].reshape(3, node_buckets, width).transpose(1, 0, 2)
    bucket_geom = (
        jnp.concatenate([facet_centroid, facet_normal], 0)
        .reshape(6, facet_buckets, width)
        .transpose(1, 0, 2)
    )
    owners = pair_owner[0, 0, :, 0]
    buckets = pair_bucket[0, 0]
    slots = pair_slot[0, 0]
    rows = buckets.shape[0]
    positions = jnp.arange(rows, dtype=jnp.int32)
    is_live = positions < pair_count[0, 0]
    live_count = jnp.sum(is_live.astype(jnp.int32))
    slot_index = slot_numbers(owners, is_live, per_owner, slot_total)
    request = (
        jnp.full((slot_total + 1,), -1, jnp.int32)
        .at[slot_index]
        .set(slots)[:-1]
        .reshape(domains, per_owner)
    )
    every_bucket = lax.all_gather(bucket_points, "dom", axis=0, tiled=True)
    point_rows = every_bucket[owners * node_buckets + slots]
    slot_acc, facet_acc = pair_loop(
        live_count,
        bucket_geom[buckets],
        point_rows,
        slot_index,
        buckets,
        is_live,
        slot_total,
        facet_buckets,
    )
    home_blocks, home_slots = (
        lax.all_to_all(
            slot_acc[:-1].reshape(domains, per_owner, 3, width),
            "dom",
            split_axis=0,
            concat_axis=0,
            tiled=True,
        ),
        lax.all_to_all(request.astype(jnp.float32), "dom", split_axis=0, concat_axis=0, tiled=True),
    )
    home_slots = home_slots.reshape(slot_total).astype(jnp.int32)
    home_blocks = home_blocks.reshape(slot_total, 3, width)
    target = jnp.where(home_slots >= 0, home_slots, node_buckets)
    bucket_force = (
        jnp.zeros((node_buckets + 1, 3, width), jnp.float32).at[target].add(home_blocks)[:-1]
    )
    node_force = (
        jnp.zeros((3, node_pos.shape[1]), jnp.float32)
        .at[:, node_order[0]]
        .add(bucket_force.transpose(1, 0, 2).reshape(3, -1))
    )
    reaction = facet_acc.transpose(1, 0, 2).reshape(3, -1) / 3.0
    for corner in range(3):
        node_force = node_force.at[:, facet_nodes[corner]].add(reaction)
    return lax.psum(node_force, "rep")


def solution(mesh):
    placed = (
        P(None, "dom"),
        P("dom", None),
        P(None, "dom"),
        P(None, "dom"),
        P(None, "dom"),
        P("rep", "dom", None),
        P("rep", "dom", None, None),
        P("rep", "dom", None),
        P("rep", "dom"),
    )
    return jax.shard_map(
        per_device, mesh=mesh, in_specs=placed, out_specs=P(None, "dom"), check_vma=False
    )
```

profile of v0, /device:TPU:0, one launch (start us, length us, event | category | flops | bytes accessed | tf_op | source)
XLA Modules:
  0.0 215.3 jit_solution(11657129899521065713)
XLA Ops:
  0.7 0.9 convert_reduce_fusion
  2.3 1.1 scatter_custom_fusion.2
  4.1 6.4 %all-to-all-start = ((f32[8,1,32]{2,1,0:T(1,128)}), f32[8,1,32]{2,1,0:T(1,128)S(1)}, u32[]{:S(2)}, u32[]{:S(2)}) async-start(f32[8,1,32]{2,1,0:T(1,128)} %convert_element_type.37), calls=%async_computation | async-start | bytes 8192 | tf_op jit(solution)/shard_map/all_to_all | solution.py:125
  12.4 1.1 copy.46
  13.5 5.5 %gather_fusion.1 = f32[2048,3]{1,0:T(8,128)S(1)} fusion(f32[3,2048]{0,1:T(8,128)S(1)} %copy.46, s32[2048]{0:T(1024)S(1)} %broadcast_clamp_fusion), kind=kCustom, calls=%fused_computation.1 | custom fusion | bytes 57344 | tf_op jit(solution)/shard_map/gather | solution.py:85
  19.3 14.8 %all_gather.3 = f32[128,3,128]{2,0,1:T(8,128)S(1)} all-gather(f32[16,3,128]{2,0,1:T(8,128)S(1)} %bitcast.77), channel_id=1, replica_groups=mesh['rep'=4,'dom'=8] {'dom'}, dimensions={0}, use_global_device_ids=true | all-gather | bytes 221184 | tf_op jit(solution)/shard_map/all_gather | solution.py:105
  36.1 62.5 %while.12 = (s32[]{:T(128)}, f32[257,3,128]{2,1,0:T(4,128)S(1)}, f32[16,3,128]{2,1,0:T(4,128)S(1)}, s32[]{:T(128)}, s32[136]{0:T(256)S(1)}, /*index=5*/f32[136,6...) while((s32[]{:T(128)}, f32[257,3,128]{2,1,0:T(4,128)S(1)}, ...), condition=%wide.region_9.10_spmd, body=%wide.region_3.9_spmd.sunk | while | flops 8012863 | bytes 3387895 | solution.py:65
  36.1 1.0 fusion.23
  38.3 0.8 scatter_fusion
  39.2 0.8 scatter_fusion.1
  40.1 1.0 fusion.23
  42.3 0.8 scatter_fusion
  43.1 0.8 scatter_fusion.1
  44.0 1.0 fusion.23
  46.2 0.8 scatter_fusion
  47.0 0.8 scatter_fusion.1
  47.9 1.0 fusion.23
  50.1 0.8 scatter_fusion
  50.9 0.8 scatter_fusion.1
  51.8 1.0 fusion.23
  54.0 0.8 scatter_fusion
  54.8 0.8 scatter_fusion.1
  55.7 1.0 fusion.23
  57.9 0.8 scatter_fusion
  58.7 0.8 scatter_fusion.1
  59.6 1.0 fusion.23
  61.8 0.8 scatter_fusion
  62.6 0.8 scatter_fusion.1
  63.5 1.0 fusion.23
  65.7 0.8 scatter_fusion
  66.5 0.8 scatter_fusion.1
  67.4 1.0 fusion.23
  69.6 0.8 scatter_fusion
  70.5 0.8 scatter_fusion.1
  71.3 1.0 fusion.23
  73.5 0.8 scatter_fusion
  74.4 0.8 scatter_fusion.1
  75.2 1.0 fusion.23
  77.4 0.8 scatter_fusion
  78.3 0.8 scatter_fusion.1
  79.1 1.0 fusion.23
  81.3 0.8 scatter_fusion
  82.2 0.8 scatter_fusion.1
  83.0 1.0 fusion.23
  85.2 0.8 scatter_fusion
  86.1 0.8 scatter_fusion.1
  86.9 1.0 fusion.23
  89.1 0.8 scatter_fusion
  90.0 0.8 scatter_fusion.1
  90.8 1.0 fusion.23
  93.0 0.8 scatter_fusion
  93.9 0.8 scatter_fusion.1
  94.7 1.0 fusion.23
  96.9 0.8 scatter_fusion
  97.8 0.8 scatter_fusion.1
  99.8 3.5 %all-to-all-start.1 = ((f32[8,32,3,128]{3,1,2,0:T(8,128)}), f32[8,32,3,128]{3,1,2,0:T(8,128)S(1)}, u32[]{:S(2)}, u32[]{:S(2)}) async-start(f32[8,32,3,128]{3,1,2,0:T(8,128)} %copy.50), calls=%async_computation.1 | async-start | bytes 786432 | tf_op jit(solution)/shard_map/all_to_all | solution.py:118
  103.5 12.3 %all-to-all-done.1 = f32[8,32,3,128]{3,1,2,0:T(8,128)S(1)} async-done(((f32[8,32,3,128]{3,1,2,0:T(8,128)}), f32[8,32,3,128]{3,1,2,0:T(8,128)S(1)}, u32[]{:S(2)}, u32[]{:S(2)}) %all-to-all-start.1) | async-done | bytes 393248 | tf_op jit(solution)/shard_map/all_to_all | solution.py:118
  116.1 8.9 %scatter_fusion.2 = f32[17,3,128]{2,1,0:T(4,128)S(1)} fusion(f32[17,3,128]{2,1,0:T(4,128)S(1)} %broadcast_in_dim.32, s32[256]{0:T(256)S(1)} %bitcast.84, f32[256,3,128]{2,1,0:T(4,128)S(1)} %copy.52), kind=kCustom, calls=%fused_computation.6 | custom fusion | flops 98304 | bytes 1180672 | tf_op jit(solution)/shard_map/scatter-add | solution.py:131
  125.3 11.7 %scatter_custom_fusion.4 = f32[3,2048]{0,1:T(8,128)S(1)} fusion(s32[2048]{0:T(1024)S(1)} %bitcast.82, f32[2048,3]{1,0:T(8,128)S(1)} %copy.53, f32[]{:T(128)} %constant.33.clone.1), kind=kCustom, calls=%fused_computation.26 | custom fusion | flops 6144 | bytes 24580 | tf_op jit(solution)/shard_map/scatter-add | solution.py:136
  137.1 11.9 %scatter_fusion.3 = f32[3,2048]{0,1:T(8,128)S(1)} fusion(f32[3,2048]{0,1:T(8,128)S(1)} %scatter_custom_fusion.4, s32[2048]{0:T(1024)S(1)} %bitcast.80, f32[2048,3]{1,0:T(8,128)S(1)} %copy.54), kind=kCustom, calls=%fused_computation.8 | custom fusion | flops 6144 | bytes 81920 | tf_op jit(solution)/shard_map/scatter-add | solution.py:140
  148.9 12.1 %scatter_fusion.4 = f32[3,2048]{0,1:T(8,128)S(1)} fusion(f32[3,2048]{0,1:T(8,128)S(1)} %scatter_fusion.3, s32[2048]{0:T(1024)S(1)} %bitcast.79, f32[2048,3]{1,0:T(8,128)S(1)} %copy.54), kind=kCustom, calls=%fused_computation.9 | custom fusion | flops 6144 | bytes 81920 | tf_op jit(solution)/shard_map/scatter-add | solution.py:140
  161.0 11.9 %scatter_fusion.5 = f32[3,2048]{0,1:T(8,128)S(1)} fusion(f32[3,2048]{0,1:T(8,128)S(1)} %scatter_fusion.4, s32[2048]{0:T(1024)S(1)} %bitcast.78, f32[2048,3]{1,0:T(8,128)S(1)} %copy.54), kind=kCustom, calls=%fused_computation.10 | custom fusion | flops 6144 | bytes 81920 | tf_op jit(solution)/shard_map/scatter-add | solution.py:140
  172.9 41.5 %psum.7 = f32[3,2048]{0,1:T(8,128)S(1)} all-reduce(f32[3,2048]{0,1:T(8,128)S(1)} %scatter_fusion.5), channel_id=1, replica_groups=mesh['rep'=4,'dom'=8] {'rep'}, use_global_device_ids=true, to_apply=%region_15.16 | all-reduce | flops 6144 | bytes 49152 | tf_op jit(solution)/shard_map/psum | solution.py:141
  214.4 0.9 copy.57
  (144 shorter events, 26.9 us)
Async XLA Ops:
  4.1 95.8 %all-to-all-start = ((f32[8,1,32]{2,1,0:T(1,128)}), f32[8,1,32]{2,1,0:T(1,128)S(1)}, u32[]{:S(2)}, u32[]{:S(2)}) async-start(f32[8,1,32]{2,1,0:T(1,128)} %convert_element_type.37), calls=%async_computation | async-start | bytes 8192 | tf_op jit(solution)/shard_map/all_to_all | solution.py:125
  13.5 20.7 %copy-start.3 = (s32[1,1,128,1]{2,3,1,0:T(1,128)S(1)}, s32[1,1,128,1]{2,3,1,0:T(1,128)}, u32[]{:S(2)}) copy-start(s32[1,1,128,1]{2,3,1,0:T(1,128)} %param.17) | copy-start | bytes 1540
  13.5 20.8 %copy-start.4 = (s32[1,1,128]{2,1,0:T(1,128)S(1)}, s32[1,1,128]{2,1,0:T(1,128)}, u32[]{:S(2)}) copy-start(s32[1,1,128]{2,1,0:T(1,128)} %param.16) | copy-start | bytes 1540
  19.3 15.8 %copy-start = (f32[3,2048]{1,0:T(4,128)S(1)}, f32[3,2048]{1,0:T(4,128)}, u32[]{:S(2)}) copy-start(f32[3,2048]{1,0:T(4,128)} %param.14) | copy-start | bytes 73732
  19.3 15.8 %copy-start.1 = (f32[3,2048]{1,0:T(4,128)S(1)}, f32[3,2048]{1,0:T(4,128)}, u32[]{:S(2)}) copy-start(f32[3,2048]{1,0:T(4,128)} %param.13) | copy-start | bytes 73732
  99.5 3.9 %copy-start.2 = (s32[3,2048]{1,0:T(4,128)S(1)}, s32[3,2048]{1,0:T(4,128)}, u32[]{:S(2)}) copy-start(s32[3,2048]{1,0:T(4,128)} %param.15) | copy-start | bytes 73732
  99.8 15.9 %all-to-all-start.1 = ((f32[8,32,3,128]{3,1,2,0:T(8,128)}), f32[8,32,3,128]{3,1,2,0:T(8,128)S(1)}, u32[]{:S(2)}, u32[]{:S(2)}) async-start(f32[8,32,3,128]{3,1,2,0:T(8,128)} %copy.50), calls=%async_computation.1 | async-start | bytes 786432 | tf_op jit(solution)/shard_map/all_to_all | solution.py:118
where the time goes:
time: 216 us; the launch traced here: 215 us
  other arithmetic  112 us (52%)
  blocking collectives  56.2 us (26%)
  local copies, waits for them, and re-layouts  13.8 us (6%)
  waiting for transfers between devices  12.3 us (6%)
  starting transfers between devices  9.82 us (5%)
  matrix products  8.35 us (4%)
    psum x1, blocking collectives, per_device(): return lax.psum(node_force, 'rep')  41.5 us
    scatter-add x3, other arithmetic, per_device(): node_force = node_force.at[:, facet_nodes[corner]].add(reaction)  35.8 us
    reduce_sum x16, other arithmetic, tile_terms(): gap = jnp.sum(normal[:, :, :, None] * delta, axis=1)  16.6 us
    all_gather x1, blocking collectives, per_device(): every_bucket = lax.all_gather(bucket_points, 'dom', axis=0, tiled=True)  14.8 us
    scatter-add x16, other arithmetic, step(): slot_acc = slot_acc.at[slot_take].add(node_term * weight[:, None, None])  12.5 us
    scatter-add x16, other arithmetic, step(): bucket_acc.at[bucket_take].add(reaction * weight[:, None, None])  12.5 us
    all_to_all x1, waiting for transfers between devices, per_device(): lax.all_to_all(slot_acc[:-1].reshape(domains, per_owner, 3, width), 'dom'...  12.3 us
    scatter-add x1, other arithmetic, per_device(): node_force = jnp.zeros((3, node_pos.shape[1]), jnp.float32).at[:, node_or...  11.7 us
  transfers between devices with their start and end apart: 2, of which 1 were waited for; matrix products, arithmetic and copies ran while one was open for 34% of the time, Pallas kernels for 0%

commit v1 on v0

--- a/solution.py
+++ b/solution.py
@@ -8,6 +8,12 @@
 STIFFNESS = 0.125
 RADIUS_SQ = 4.0
 pair_block = 8
+
+
+def add_all(x, mesh_axis):
+    shards = lax.all_gather(x, mesh_axis, axis=0, tiled=False)
+    total = shards.sum(axis=0)
+    return total
 
 
 def tile_terms(facet_geom, node_points):
@@ -138,7 +144,7 @@
     reaction = facet_acc.transpose(1, 0, 2).reshape(3, -1) / 3.0
     for corner in range(3):
         node_force = node_force.at[:, facet_nodes[corner]].add(reaction)
-    return lax.psum(node_force, "rep")
+    return add_all(node_force, "rep")
 
 
 def solution(mesh):

time: 216 us -> 184 us (0.85)
  blocking collectives: 56.2 us -> 24.4 us
    psum x1 -> x0, blocking collectives: 41.5 us -> none  [per_device(): return lax.psum(node_force, 'rep')]
    all_gather x0 -> x1, blocking collectives: none -> 9.59 us  [add_all(): shards = lax.all_gather(x, mesh_axis, axis=0, tiled=False)]
  transfers between devices with their start and end apart: 2 -> 2, of which waited for: 1 -> 1; matrix products, arithmetic and copies ran while one was open for 34% -> 40% of each run, Pallas kernels for 0% -> 0%
where the time goes in v1:
time: 184 us; the launch traced here: 183 us
  other arithmetic  113 us (61%)
  blocking collectives  24.4 us (13%)
  local copies, waits for them, and re-layouts  13.1 us (7%)
  waiting for transfers between devices  12.3 us (7%)
  starting transfers between devices  9.82 us (5%)
  matrix products  8.35 us (5%)
    scatter-add x3, other arithmetic, per_device(): node_force = node_force.at[:, facet_nodes[corner]].add(reaction)  35.6 us
    reduce_sum x16, other arithmetic, tile_terms(): gap = jnp.sum(normal[:, :, :, None] * delta, axis=1)  16.6 us
    all_gather x1, blocking collectives, per_device(): every_bucket = lax.all_gather(bucket_points, 'dom', axis=0, tiled=True)  14.8 us
    scatter-add x16, other arithmetic, step(): slot_acc = slot_acc.at[slot_take].add(node_term * weight[:, None, None])  12.5 us
    scatter-add x16, other arithmetic, step(): bucket_acc.at[bucket_take].add(reaction * weight[:, None, None])  12.5 us
    all_to_all x1, waiting for transfers between devices, per_device(): lax.all_to_all(slot_acc[:-1].reshape(domains, per_owner, 3, width), 'dom'...  12.3 us
    scatter-add x1, other arithmetic, per_device(): node_force = jnp.zeros((3, node_pos.shape[1]), jnp.float32).at[:, node_or...  11.7 us
    all_gather x1, blocking collectives, add_all(): shards = lax.all_gather(x, mesh_axis, axis=0, tiled=False)  9.59 us
  transfers between devices with their start and end apart: 2, of which 1 were waited for; matrix products, arithmetic and copies ran while one was open for 40% of the time, Pallas kernels for 0%

profile of v1, /device:TPU:0, one launch (start us, length us, event | category | flops | bytes accessed | tf_op | source)
XLA Modules:
  0.0 183.3 jit_solution(5086986562550528832)
XLA Ops:
  0.7 0.9 convert_reduce_fusion
  2.3 1.1 scatter_custom_fusion.2
  4.1 6.4 %all-to-all-start = ((f32[8,1,32]{2,1,0:T(1,128)}), f32[8,1,32]{2,1,0:T(1,128)S(1)}, u32[]{:S(2)}, u32[]{:S(2)}) async-start(f32[8,1,32]{2,1,0:T(1,128)} %convert_element_type.37), calls=%async_computation | async-start | bytes 8192 | tf_op jit(solution)/shard_map/all_to_all | solution.py:131
  12.4 1.1 copy.47
  13.5 5.5 %gather_fusion.1 = f32[2048,3]{1,0:T(8,128)S(1)} fusion(f32[3,2048]{0,1:T(8,128)S(1)} %copy.47, s32[2048]{0:T(1024)S(1)} %broadcast_clamp_fusion), kind=kCustom, calls=%fused_computation.1 | custom fusion | bytes 57344 | tf_op jit(solution)/shard_map/gather | solution.py:91
  19.3 14.8 %all_gather.9 = f32[128,3,128]{2,0,1:T(8,128)S(1)} all-gather(f32[16,3,128]{2,0,1:T(8,128)S(1)} %bitcast.79), channel_id=1, replica_groups=mesh['rep'=4,'dom'=8] {'dom'}, dimensions={0}, use_global_device_ids=true | all-gather | bytes 221184 | tf_op jit(solution)/shard_map/all_gather | solution.py:111
  36.1 62.5 %while.12 = (s32[]{:T(128)}, f32[257,3,128]{2,1,0:T(4,128)S(1)}, f32[16,3,128]{2,1,0:T(4,128)S(1)}, s32[]{:T(128)}, s32[136]{0:T(256)S(1)}, /*index=5*/f32[136,6...) while((s32[]{:T(128)}, f32[257,3,128]{2,1,0:T(4,128)S(1)}, ...), condition=%wide.region_9.10_spmd, body=%wide.region_3.9_spmd.sunk | while | flops 8012863 | bytes 3387895 | solution.py:71
  36.1 1.0 fusion.23
  38.3 0.8 scatter_fusion
  39.2 0.8 scatter_fusion.1
  40.1 1.0 fusion.23
  42.3 0.8 scatter_fusion
  43.1 0.8 scatter_fusion.1
  44.0 1.0 fusion.23
  46.2 0.8 scatter_fusion
  47.0 0.8 scatter_fusion.1
  47.9 1.0 fusion.23
  50.1 0.8 scatter_fusion
  50.9 0.8 scatter_fusion.1
  51.8 1.0 fusion.23
  54.0 0.8 scatter_fusion
  54.8 0.8 scatter_fusion.1
  55.7 1.0 fusion.23
  57.9 0.8 scatter_fusion
  58.7 0.8 scatter_fusion.1
  59.6 1.0 fusion.23
  61.8 0.8 scatter_fusion
  62.6 0.8 scatter_fusion.1
  63.5 1.0 fusion.23
  65.7 0.8 scatter_fusion
  66.5 0.8 scatter_fusion.1
  67.4 1.0 fusion.23
  69.6 0.8 scatter_fusion
  70.5 0.8 scatter_fusion.1
  71.3 1.0 fusion.23
  73.5 0.8 scatter_fusion
  74.4 0.8 scatter_fusion.1
  75.2 1.0 fusion.23
  77.4 0.8 scatter_fusion
  78.3 0.8 scatter_fusion.1
  79.1 1.0 fusion.23
  81.3 0.8 scatter_fusion
  82.2 0.8 scatter_fusion.1
  83.0 1.0 fusion.23
  85.2 0.8 scatter_fusion
  86.1 0.8 scatter_fusion.1
  86.9 1.0 fusion.23
  89.1 0.8 scatter_fusion
  90.0 0.8 scatter_fusion.1
  90.8 1.0 fusion.23
  93.0 0.8 scatter_fusion
  93.9 0.8 scatter_fusion.1
  94.7 1.0 fusion.23
  96.9 0.8 scatter_fusion
  97.8 0.8 scatter_fusion.1
  98.7 0.8 copy.51
  99.8 3.5 %all-to-all-start.1 = ((f32[8,32,3,128]{3,1,2,0:T(8,128)}), f32[8,32,3,128]{3,1,2,0:T(8,128)S(1)}, u32[]{:S(2)}, u32[]{:S(2)}) async-start(f32[8,32,3,128]{3,1,2,0:T(8,128)} %copy.51), calls=%async_computation.1 | async-start | bytes 786432 | tf_op jit(solution)/shard_map/all_to_all | solution.py:124
  103.5 12.3 %all-to-all-done.1 = f32[8,32,3,128]{3,1,2,0:T(8,128)S(1)} async-done(((f32[8,32,3,128]{3,1,2,0:T(8,128)}), f32[8,32,3,128]{3,1,2,0:T(8,128)S(1)}, u32[]{:S(2)}, u32[]{:S(2)}) %all-to-all-start.1) | async-done | bytes 393248 | tf_op jit(solution)/shard_map/all_to_all | solution.py:124
  116.1 8.9 %scatter_fusion.2 = f32[17,3,128]{2,1,0:T(4,128)S(1)} fusion(f32[17,3,128]{2,1,0:T(4,128)S(1)} %broadcast_in_dim.32, s32[256]{0:T(256)S(1)} %bitcast.86, f32[256,3,128]{2,1,0:T(4,128)S(1)} %copy.53), kind=kCustom, calls=%fused_computation.6 | custom fusion | flops 98304 | bytes 1180672 | tf_op jit(solution)/shard_map/scatter-add | solution.py:137
  125.3 11.7 %scatter_custom_fusion.4 = f32[3,2048]{0,1:T(8,128)S(1)} fusion(s32[2048]{0:T(1024)S(1)} %bitcast.84, f32[2048,3]{1,0:T(8,128)S(1)} %copy.54, f32[]{:T(128)} %constant.33.clone.1), kind=kCustom, calls=%fused_computation.26 | custom fusion | flops 6144 | bytes 24580 | tf_op jit(solution)/shard_map/scatter-add | solution.py:142
  137.1 11.9 %scatter_fusion.3 = f32[3,2048]{0,1:T(8,128)S(1)} fusion(f32[3,2048]{0,1:T(8,128)S(1)} %scatter_custom_fusion.4, s32[2048]{0:T(1024)S(1)} %bitcast.82, f32[2048,3]{1,0:T(8,128)S(1)} %copy.55), kind=kCustom, calls=%fused_computation.8 | custom fusion | flops 6144 | bytes 81920 | tf_op jit(solution)/shard_map/scatter-add | solution.py:146
  148.9 11.9 %scatter_fusion.4 = f32[3,2048]{0,1:T(8,128)S(1)} fusion(f32[3,2048]{0,1:T(8,128)S(1)} %scatter_fusion.3, s32[2048]{0:T(1024)S(1)} %bitcast.81, f32[2048,3]{1,0:T(8,128)S(1)} %copy.55), kind=kCustom, calls=%fused_computation.9 | custom fusion | flops 6144 | bytes 81920 | tf_op jit(solution)/shard_map/scatter-add | solution.py:146
  160.8 11.9 %scatter_fusion.5 = f32[3,2048]{0,1:T(8,128)S(1)} fusion(f32[3,2048]{0,1:T(8,128)S(1)} %scatter_fusion.4, s32[2048]{0:T(1024)S(1)} %bitcast.80, f32[2048,3]{1,0:T(8,128)S(1)} %copy.55), kind=kCustom, calls=%fused_computation.10 | custom fusion | flops 6144 | bytes 81920 | tf_op jit(solution)/shard_map/scatter-add | solution.py:146
  173.0 9.6 %all-gather.1 = f32[4,3,2048]{2,1,0:T(4,128)S(1)} all-gather(f32[1,3,2048]{2,1,0:T(4,128)S(1)} %copy.58), channel_id=2, replica_groups=mesh['rep'=4,'dom'=8] {'rep'}, dimensions={0}, use_global_device_ids=true | all-gather | bytes 122880 | tf_op jit(solution)/shard_map/all_gather | solution.py:14
  (145 shorter events, 27.1 us)
Async XLA Ops:
  4.1 95.8 %all-to-all-start = ((f32[8,1,32]{2,1,0:T(1,128)}), f32[8,1,32]{2,1,0:T(1,128)S(1)}, u32[]{:S(2)}, u32[]{:S(2)}) async-start(f32[8,1,32]{2,1,0:T(1,128)} %convert_element_type.37), calls=%async_computation | async-start | bytes 8192 | tf_op jit(solution)/shard_map/all_to_all | solution.py:131
  13.5 20.7 %copy-start.3 = (s32[1,1,128,1]{2,3,1,0:T(1,128)S(1)}, s32[1,1,128,1]{2,3,1,0:T(1,128)}, u32[]{:S(2)}) copy-start(s32[1,1,128,1]{2,3,1,0:T(1,128)} %param.17) | copy-start | bytes 1540
  13.5 20.8 %copy-start.4 = (s32[1,1,128]{2,1,0:T(1,128)S(1)}, s32[1,1,128]{2,1,0:T(1,128)}, u32[]{:S(2)}) copy-start(s32[1,1,128]{2,1,0:T(1,128)} %param.16) | copy-start | bytes 1540
  19.3 15.8 %copy-start = (f32[3,2048]{1,0:T(4,128)S(1)}, f32[3,2048]{1,0:T(4,128)}, u32[]{:S(2)}) copy-start(f32[3,2048]{1,0:T(4,128)} %param.14) | copy-start | bytes 73732
  19.3 15.8 %copy-start.1 = (f32[3,2048]{1,0:T(4,128)S(1)}, f32[3,2048]{1,0:T(4,128)}, u32[]{:S(2)}) copy-start(f32[3,2048]{1,0:T(4,128)} %param.13) | copy-start | bytes 73732
  99.5 3.9 %copy-start.2 = (s32[3,2048]{1,0:T(4,128)S(1)}, s32[3,2048]{1,0:T(4,128)}, u32[]{:S(2)}) copy-start(s32[3,2048]{1,0:T(4,128)} %param.15) | copy-start | bytes 73732
  99.8 15.9 %all-to-all-start.1 = ((f32[8,32,3,128]{3,1,2,0:T(8,128)}), f32[8,32,3,128]{3,1,2,0:T(8,128)S(1)}, u32[]{:S(2)}, u32[]{:S(2)}) async-start(f32[8,32,3,128]{3,1,2,0:T(8,128)} %copy.51), calls=%async_computation.1 | async-start | bytes 786432 | tf_op jit(solution)/shard_map/all_to_all | solution.py:124
